TPU v7x, 32 devices: a whole 2x2x4 slice. The times are simulated.
32 devices in a mesh: ctx: 8 (over z, y), head: 4 (over x, core).
Axes of the slice: x: 2, y: 2, z: 4, core: 2. Of those that a mesh axis runs over, the one named last changes fastest.
Arguments:
- queries: bfloat16 [8192, 16, 128], P('ctx', 'head'), may hold values from -240 to 240, as said below
- lookup_arrays: bfloat16 [8192, 4, 128], P('ctx', 'head'), may hold values from -6 to 6
- content_arrays: bfloat16 [8192, 4, 128], P('ctx', 'head'), may hold values from -6 to 6
- selection: int32 [16, 4, 6], P('ctx', 'head'), may hold values from 0 to 15, as said below
- final_mapping: bfloat16 [2048, 4096], P('head'), may hold values from -0.125 to 0.125
Outputs:
- layer_out: bfloat16 [8192, 4096], P(('ctx', 'head'))
Inputs may be any that keep to these rules, and one draw needn't show every extreme that they name: `queries`: entries lie within -240 and 240. selection[b, h, :] holds 6 block numbers no larger than b; those smaller than b are distinct, and an entry equal to b names nothing. For each KV head and each index c of ctx, the selections of the 2 blocks held at c name, among the blocks held at any one index below c, at most one distinct block, and this bound is met.
All inputs are finite; a program needn't handle non-finite values.
Results may differ from a plain program's by a relative error of at most 0.01.
Values may be sent and summed in bfloat16 or wider, within the bound.
A program may use at most 128 MiB of HBM per device.

v0:
```python
import jax
import jax.numpy as jnp
from jax import lax
from jax.sharding import PartitionSpec as P


def attend_block(operands):
    query_block, key_block, value_block, permitted_mask = operands
    block_size = query_block.shape[0]
    scaling = query_block.shape[-1] ** (-0.5)
    affinity_grid = (
        jnp.einsum("qgd,skd->gqsk", query_block, key_block, preferred_element_type=jnp.float32)
        * scaling
    )
    causal = jnp.arange(block_size)[:, None] >= jnp.arange(block_size)[None, :]
    slot_count = key_block.shape[0]
    own_slot = jnp.arange(slot_count) == slot_count - 1
    allowed = permitted_mask[:, None, None] & (~own_slot[:, None, None] | causal[None])
    allowed = allowed.transpose(1, 0, 2)[None]
    affinity_grid = jnp.where(allowed, affinity_grid, -jnp.inf)
    row_peak = jnp.max(affinity_grid, axis=(2, 3), keepdims=True)
    weights = jnp.exp(affinity_grid - row_peak)
    totals = jnp.sum(weights, axis=(2, 3))
    mixed_result = jnp.einsum(
        "gqsk,skd->qgd",
        weights.astype(jnp.bfloat16),
        value_block,
        preferred_element_type=jnp.float32,
    )
    return (mixed_result / totals.T[:, :, None]).astype(jnp.bfloat16)


def body(queries, lookup_arrays, content_arrays, selection, final_mapping):
    ctx_count = lax.axis_size("ctx")
    position = lax.axis_index("ctx")
    blocks_here = selection.shape[0]
    tokens_here = queries.shape[0]
    block_size = tokens_here // blocks_here
    askers_per_leader = queries.shape[1]
    head_dim = queries.shape[2]
    stacked = jnp.stack(
        [
            lookup_arrays.reshape(blocks_here, block_size, head_dim),
            content_arrays.reshape(blocks_here, block_size, head_dim),
        ]
    )
    chosen = selection[:, 0, :]
    holder_list = chosen // blocks_here
    distant = holder_list <= position - 1
    peer_ids = jnp.arange(ctx_count, dtype=jnp.int32)
    last_id = ctx_count * blocks_here - 1
    matches = distant[:, :, None] & (holder_list[:, :, None] == peer_ids[None, None, :])
    wanted_ids = jnp.max(jnp.where(matches, chosen[:, :, None], -1), axis=(0, 1))
    coded = jnp.where(wanted_ids >= 0, last_id - wanted_ids, -1).astype(jnp.int32)
    received = lax.all_to_all(
        coded.reshape(ctx_count, 1), "ctx", split_axis=0, concat_axis=0, tiled=True
    ).reshape(ctx_count)
    requested = last_id - received
    local_index = jnp.clip(requested - position * blocks_here, 0, blocks_here - 1)
    packed = jnp.take(stacked, local_index, axis=1)
    arrived = lax.all_to_all(packed, "ctx", split_axis=1, concat_axis=1, tiled=True)
    block_pool = jnp.concatenate([stacked, arrived], axis=1)
    block_ids = position * blocks_here + jnp.arange(blocks_here, dtype=jnp.int32)
    slot_ids = jnp.concatenate([chosen, block_ids[:, None]], axis=1)
    permitted_mask = jnp.concatenate(
        [chosen != block_ids[:, None], jnp.ones((blocks_here, 1), jnp.bool_)], axis=1
    )
    slot_owner = slot_ids // blocks_here
    pool_index = jnp.where(
        slot_owner == position, slot_ids - position * blocks_here, blocks_here + slot_owner
    )
    selected = jnp.take(block_pool, pool_index, axis=1)
    asking_lines = queries.reshape(blocks_here, block_size, askers_per_leader, head_dim)
    mixed_result = lax.map(attend_block, (asking_lines, selected[0], selected[1], permitted_mask))
    flat_rows = mixed_result.reshape(tokens_here, askers_per_leader * head_dim)

    def project():
        part_rows = lax.slice_in_dim(
            flat_rows, 0, lax.axis_size("head") * (tokens_here // lax.axis_size("head")), axis=0
        )
        return jnp.dot(part_rows, final_mapping, preferred_element_type=jnp.float32)

    summed = lax.psum_scatter(
        project().astype(jnp.bfloat16), "head", scatter_dimension=0, tiled=True
    ).astype(jnp.float32)
    return summed.astype(jnp.bfloat16)


def solution(mesh):
    in_specs = (
        P("ctx", "head", None),
        P("ctx", "head", None),
        P("ctx", "head", None),
        P("ctx", "head", None),
        P("head", None),
    )
    out_specs = P(("ctx", "head"), None)
    return jax.shard_map(body, mesh=mesh, in_specs=in_specs, out_specs=out_specs, check_vma=False)
```

profile of v0, /device:TPU:0, one launch (start us, length us, event | category | flops | bytes accessed | tf_op | source)
XLA Modules:
  0.0 254.1 jit_solution(15843986675841685980)
XLA Ops:
  6.5 0.8 copy.48
  7.3 0.8 broadcast_compare_fusion.1
  8.1 0.1 copy.47
  8.1 0.1 copy.46
  8.3 0.1 fusion.26
  8.4 0.7 copy.49
  9.0 7.3 %all-to-all-start = ((s32[8,1,1]{2,1,0:T(1,128)}), s32[8,1,1]{2,1,0:T(1,128)S(1)}, u32[]{:S(2)}, u32[]{:S(2)}) async-start(s32[8,1,1]{2,1,0:T(1,128)} %copy.49), calls=%async_computation | async-start | bytes 8192 | tf_op jit(solution)/shard_map/all_to_all | solution.py:55
  16.4 1.1 pad_maximum_fusion.1
  17.5 5.3 %all-to-all-done = s32[8,1,1]{2,1,0:T(1,128)S(1)} async-done(((s32[8,1,1]{2,1,0:T(1,128)}), s32[8,1,1]{2,1,0:T(1,128)S(1)}, u32[]{:S(2)}, u32[]{:S(2)}) %all-to-all-start) | async-done | bytes 64 | tf_op jit(solution)/shard_map/all_to_all | solution.py:55
  22.8 0.2 clamp_reduce_fusion
  23.0 1.0 gather_fusion
  24.0 0.0 copy-start.4
  24.0 0.0 copy-start.2
  24.0 0.0 copy-start.3
  24.0 1.6 select_bitcast_fusion
  25.6 3.6 %all-to-all-start.1 = ((bf16[2,8,512,128]{3,2,0,1:T(8,128)(2,1)}), bf16[2,8,512,128]{3,2,0,1:T(8,128)(2,1)S(1)}, u32[]{:S(2)}, u32[]{:S(2)}) async-start(bf16[2,8,512,128]{3,2,0,1:T(8,128)(2,1)} %select_bitcast_fusion), calls=%async_computation.1 | async-start | bytes 4194304 | tf_op jit(solution)/shard_map/all_to_all | solution.py:61
  29.2 0.0 reduce-scatter.2.cloned.1.call-start
  29.3 0.0 copy-done.4
  29.3 0.1 compare_select_fusion
  29.4 0.1 reshape.329
  29.5 0.1 compare_and_fusion.1
  29.6 46.6 %all-to-all-done.1 = bf16[2,8,512,128]{3,2,0,1:T(8,128)(2,1)S(1)} async-done(((bf16[2,8,512,128]{3,2,0,1:T(8,128)(2,1)}), bf16[2,8,512,128]{3,2,0,1:T(8,128)(2,1)S(1)}, u32[]{:S(2)}, u32[]{:S(2)}) %all-to-all-start.1) | async-done | bytes 2097184 | tf_op jit(solution)/shard_map/all_to_all | solution.py:61
  76.2 0.2 pad_maximum_fusion
  76.5 0.2 copy.52
  76.7 2.9 %gather_fusion.1 = bf16[14,2,512,128]{3,2,1,0:T(8,128)(2,1)} fusion(bf16[2,10,512,128]{3,2,1,0:T(8,128)(2,1)S(1)} %copy.52, s32[1024]{0:T(1024)S(1)} %pad_clamp_fusion), kind=kCustom, calls=%fused_computation.1 | custom fusion | bytes 7340088 | tf_op jit(solution)/shard_map/jit(_take)/gather | solution.py:72
  79.6 2.4 fusion.23
  82.0 0.0 copy-start
  82.0 2.3 slice_bitcast_fusion
  84.3 83.4 %while.10 = (s32[]{:T(128)}, bf16[2,512,4,128]{3,2,1,0:T(4,128)(2,1)S(1)}, bf16[2,7,512,128]{3,2,1,0:T(8,128)(2,1)}, pred[2,7]{1,0:T(4,128)(4,1)S(1)}, bf16[2,7,...) while((s32[]{:T(128)}, bf16[2,512,4,128]{3,2,1,0:T(4,128)(2,1)S(1)}, ...), condition=%wide.region_4.5_spmd, body=%wide.region_1.4_spmd.sunk | while | flops 3843289088 | bytes 109355664 | solution.py:74
  84.3 0.1 iota_compare_fusion.2
  84.4 1.1 or_and_fusion.2
  85.5 0.2 constant_dynamic-slice_fusion.2
  85.7 13.3 %fusion.38 = (f32[4,512]{1,0:T(4,128)S(1)}, f32[7,512,512,4]{2,1,3,0:T(8,128)}) fusion(pred[512,7,512]{0,2,1:T(8,128)(4,1)S(1)} %or_and_fusion.2, bf16[1,512,4,128]{3,2,1,0:T(4,128)(2,1)S(1)} %constant_dynamic-slice_fusion.2, bf16[2,7,512,128]{3,2,1,0:T(8,128)(2,1)} %get-tuple-element.146, s32[]{:T(128)} %get-tuple-element.135), kind=kOutput, calls=%fused_computation.6.clone.1 | convolution fusion | flops 1901066240 | bytes 32645632 | tf_op jit(solution)/shard_map/while/body/eval_jaxpr/qgd,skd->gqsk/dot_general | solution.py:12
  99.0 12.9 %fusion.39 = f32[4,512]{1,0:T(4,128)S(1)} fusion(f32[7,512,512,4]{2,1,3,0:T(8,128)} %get-tuple-element.126, f32[4,512]{1,0:T(4,128)S(1)} %get-tuple-element.127, pred[512,7,512]{0,2,1:T(8,128)(4,1)S(1)} %or_and_fusion.2), kind=kLoop, calls=%fused_computation.4.clone.1 | loop fusion | flops 29358080 | bytes 31211520 | tf_op jit(solution)/shard_map/while/body/eval_jaxpr/reduce_sum | solution.py:23
  111.9 13.5 %fusion.40 = bf16[1,512,4,128]{1,3,2,0:T(8,128)(2,1)S(1)} fusion(f32[7,512,512,4]{2,1,3,0:T(8,128)} %get-tuple-element.126, f32[4,512]{1,0:T(4,128)S(1)} %get-tuple-element.127, pred[512,7,512]{0,2,1:T(8,128)(4,1)S(1)} %or_and_fusion.2, bf16[2,7,512,128]{3,2,1,0:T(8,128)(2,1)S(1)} %copy-done.1, s32[]{:T(128)} %get-tuple-element.135, ...), kind=kOutput, calls=%fused_computation.13.clone.1 | convolution fusion | flops 1908932608 | bytes 32653316 | tf_op jit(solution)/shard_map/while/body/eval_jaxpr/gqsk,skd->qgd/dot_general | solution.py:24
  125.5 0.3 copy.83
  125.8 0.2 constant_dynamic-update-slice_fusion.2
  126.0 0.1 iota_compare_fusion.2
  126.2 1.1 or_and_fusion.2
  127.2 0.2 constant_dynamic-slice_fusion.2
  127.4 13.3 %fusion.38 = (f32[4,512]{1,0:T(4,128)S(1)}, f32[7,512,512,4]{2,1,3,0:T(8,128)}) fusion(pred[512,7,512]{0,2,1:T(8,128)(4,1)S(1)} %or_and_fusion.2, bf16[1,512,4,128]{3,2,1,0:T(4,128)(2,1)S(1)} %constant_dynamic-slice_fusion.2, bf16[2,7,512,128]{3,2,1,0:T(8,128)(2,1)} %get-tuple-element.146, s32[]{:T(128)} %get-tuple-element.135), kind=kOutput, calls=%fused_computation.6.clone.1 | convolution fusion | flops 1901066240 | bytes 32645632 | tf_op jit(solution)/shard_map/while/body/eval_jaxpr/qgd,skd->gqsk/dot_general | solution.py:12
  140.8 12.9 %fusion.39 = f32[4,512]{1,0:T(4,128)S(1)} fusion(f32[7,512,512,4]{2,1,3,0:T(8,128)} %get-tuple-element.126, f32[4,512]{1,0:T(4,128)S(1)} %get-tuple-element.127, pred[512,7,512]{0,2,1:T(8,128)(4,1)S(1)} %or_and_fusion.2), kind=kLoop, calls=%fused_computation.4.clone.1 | loop fusion | flops 29358080 | bytes 31211520 | tf_op jit(solution)/shard_map/while/body/eval_jaxpr/reduce_sum | solution.py:23
  153.7 13.5 %fusion.40 = bf16[1,512,4,128]{1,3,2,0:T(8,128)(2,1)S(1)} fusion(f32[7,512,512,4]{2,1,3,0:T(8,128)} %get-tuple-element.126, f32[4,512]{1,0:T(4,128)S(1)} %get-tuple-element.127, pred[512,7,512]{0,2,1:T(8,128)(4,1)S(1)} %or_and_fusion.2, bf16[2,7,512,128]{3,2,1,0:T(8,128)(2,1)S(1)} %copy-done.1, s32[]{:T(128)} %get-tuple-element.135, ...), kind=kOutput, calls=%fused_computation.13.clone.1 | convolution fusion | flops 1908932608 | bytes 32653316 | tf_op jit(solution)/shard_map/while/body/eval_jaxpr/gqsk,skd->qgd/dot_general | solution.py:24
  167.2 0.3 copy.83
  167.5 0.2 constant_dynamic-update-slice_fusion.2
  167.8 8.9 %convolution_convert_fusion = bf16[1024,4096]{1,0:T(8,128)(2,1)} fusion(bf16[512,4096]{1,0:T(8,128)(2,1)} %param.11, bf16[128,8,4,128]{3,2,1,0:T(4,128)(2,1)S(1)} %bitcast.113), kind=kOutput, calls=%fused_computation.28 | convolution fusion | flops 4299161600 | bytes 13631488 | tf_op jit(solution)/shard_map/dot_general | solution.py:81
  176.7 0.0 reduce-scatter.2.cloned.1.call-update
  176.7 70.6 %reduce-scatter.2.cloned.1.call-done = bf16[256,4096]{1,0:T(8,128)(2,1)} async-done(((bf16[1024,4096]{1,0:T(8,128)(2,1)}), bf16[256,4096]{1,0:T(8,128)(2,1)}) %reduce-scatter.2.cloned.1.call-update) | async-done | bytes 2097168 | tf_op jit(solution)/shard_map/reduce_scatter | solution.py:83
  (24 shorter events, 0.1 us)
Async XLA Ops:
  9.0 13.7 %all-to-all-start = ((s32[8,1,1]{2,1,0:T(1,128)}), s32[8,1,1]{2,1,0:T(1,128)S(1)}, u32[]{:S(2)}, u32[]{:S(2)}) async-start(s32[8,1,1]{2,1,0:T(1,128)} %copy.49), calls=%async_computation | async-start | bytes 8192 | tf_op jit(solution)/shard_map/all_to_all | solution.py:55
  24.0 5.3 %copy-start.4 = (s32[2,1,6]{2,1,0:T(1,128)S(1)}, s32[2,1,6]{2,1,0:T(1,128)}, u32[]{:S(2)}) copy-start(s32[2,1,6]{2,1,0:T(1,128)} %param.10) | copy-start | bytes 148
  24.0 52.2 %copy-start.2 = (bf16[1024,1,128]{2,0,1:T(8,128)(2,1)S(1)}, bf16[1024,1,128]{2,0,1:T(8,128)(2,1)}, u32[]{:S(2)}) copy-start(bf16[1024,1,128]{2,0,1:T(8,128)(2,1)} %param.9) | copy-start | bytes 786436
  24.0 52.2 %copy-start.3 = (bf16[1024,1,128]{2,0,1:T(8,128)(2,1)S(1)}, bf16[1024,1,128]{2,0,1:T(8,128)(2,1)}, u32[]{:S(2)}) copy-start(bf16[1024,1,128]{2,0,1:T(8,128)(2,1)} %param.8) | copy-start | bytes 786436
  25.6 50.6 %all-to-all-start.1 = ((bf16[2,8,512,128]{3,2,0,1:T(8,128)(2,1)}), bf16[2,8,512,128]{3,2,0,1:T(8,128)(2,1)S(1)}, u32[]{:S(2)}, u32[]{:S(2)}) async-start(bf16[2,8,512,128]{3,2,0,1:T(8,128)(2,1)} %select_bitcast_fusion), calls=%async_computation.1 | async-start | bytes 4194304 | tf_op jit(solution)/shard_map/all_to_all | solution.py:61
  29.2 218.1 %reduce-scatter.2.cloned.1.call-start = ((), (), s32[]{:S(2)}) async-start(), calls=%async_computation.3 | async-start | bytes 10485760 | tf_op jit(solution)/shard_map/reduce_scatter | solution.py:83
  82.0 2.3 copy-start
  82.0 2.3 copy-start.5
  99.0 12.9 %copy-start.1 = (bf16[2,7,512,128]{3,2,1,0:T(8,128)(2,1)S(1)}, bf16[2,7,512,128]{3,2,1,0:T(8,128)(2,1)}, u32[]{:S(2)}) copy-start(bf16[2,7,512,128]{3,2,1,0:T(8,128)(2,1)} %get-tuple-element.144) | copy-start | bytes 5505028 | tf_op jit(solution)/shard_map/while
  140.8 12.9 %copy-start.1 = (bf16[2,7,512,128]{3,2,1,0:T(8,128)(2,1)S(1)}, bf16[2,7,512,128]{3,2,1,0:T(8,128)(2,1)}, u32[]{:S(2)}) copy-start(bf16[2,7,512,128]{3,2,1,0:T(8,128)(2,1)} %get-tuple-element.144) | copy-start | bytes 5505028 | tf_op jit(solution)/shard_map/while
Sparse Core Ops, SparseCore 0:
  176.8 70.4 reduce-scatter.1
where the time goes:
time: 255 us; the launch traced here: 254 us
  waiting for transfers between devices  123 us (48%)
  matrix products  62.6 us (25%)
  other arithmetic  34.7 us (14%)
  between operations  13.6 us (5%)
  starting transfers between devices  11 us (4%)
  local copies, waits for them, and re-layouts  9.59 us (4%)
    reduce_scatter x1, waiting for transfers between devices, body(): lax.psum_scatter(project().astype(jnp.bfloat16), 'head', scatter_dimensio...  70.6 us
    all_to_all x1, waiting for transfers between devices, body(): lax.all_to_all(packed, 'ctx', split_axis=1, concat_axis=1, tiled=True)  46.6 us
    dot_general x2, matrix products, attend_block(): jnp.einsum('gqsk,skd->qgd', weights.astype(jnp.bfloat16), value_block, pr...  27.1 us
    dot_general x2, matrix products, attend_block(): jnp.einsum('qgd,skd->gqsk', query_block, key_block, preferred_element_typ...  26.6 us
    reduce_sum x2, other arithmetic, attend_block(): totals = jnp.sum(weights, axis=(2, 3))  25.8 us
    dot_general x1, matrix products, project(): return jnp.dot(part_rows, final_mapping, preferred_element_type=jnp.float32)  8.92 us
    all_to_all x1, starting transfers between devices, body(): lax.all_to_all(coded.reshape(ctx_count, 1), 'ctx', split_axis=0, concat_a...  7.31 us
    all_to_all x1, waiting for transfers between devices, body(): lax.all_to_all(coded.reshape(ctx_count, 1), 'ctx', split_axis=0, concat_a...  5.29 us
  transfers between devices with their start and end apart: 3, of which 3 were waited for; matrix products, arithmetic and copies ran while one was open for 1% of the time, Pallas kernels for 0%

commit v1 on v0

--- a/solution.py
+++ b/solution.py
@@ -58,7 +58,19 @@
     requested = last_id - received
     local_index = jnp.clip(requested - position * blocks_here, 0, blocks_here - 1)
     packed = jnp.take(stacked, local_index, axis=1)
-    arrived = lax.all_to_all(packed, "ctx", split_axis=1, concat_axis=1, tiled=True)
+    ways, here = (lax.axis_size("ctx"), lax.axis_index("ctx"))
+    width = packed.shape[1] // ways
+    shape = list(packed.shape)
+    shape[1] = width
+    height = shape[1]
+    shape[1] = height * ways
+    full = jnp.zeros(shape, packed.dtype)
+    for mask in range(ways):
+        part = lax.dynamic_slice_in_dim(packed, (here ^ mask) * width, width, axis=1)
+        if mask:
+            part = lax.ppermute(part, "ctx", [(d, d ^ mask) for d in range(ways)])
+        full = lax.dynamic_update_slice_in_dim(full, part, (here ^ mask) * height, axis=1)
+    arrived = full
     block_pool = jnp.concatenate([stacked, arrived], axis=1)
     block_ids = position * blocks_here + jnp.arange(blocks_here, dtype=jnp.int32)
     slot_ids = jnp.concatenate([chosen, block_ids[:, None]], axis=1)

time: 255 us -> 255 us (level)
  waiting for transfers between devices: 123 us -> 113 us
  starting transfers between devices: 11 us -> 17.3 us
  local copies, waits for them, and re-layouts: 9.59 us -> 12.2 us
    all_to_all x1 -> x0, waiting for transfers between devices: 46.6 us -> none  [body(): lax.all_to_all(packed, 'ctx', split_axis=1, concat_axis=1, tiled=True)]
    ppermute x0 -> x7, waiting for transfers between devices: none -> 31.3 us  [body(): part = lax.ppermute(part, 'ctx', [(d, d ^ mask) for d in range(ways)])]
    ppermute x0 -> x7, starting transfers between devices: none -> 9.95 us  [body(): part = lax.ppermute(part, 'ctx', [(d, d ^ mask) for d in range(ways)])]
    reduce_scatter x1, waiting for transfers between devices: 70.6 us -> 77.5 us  [body(): lax.psum_scatter(project().astype(jnp.bfloat16), 'head', scatter_dimensio...]
    all_to_all x1 -> x0, starting transfers between devices: 3.6 us -> none  [body(): lax.all_to_all(packed, 'ctx', split_axis=1, concat_axis=1, tiled=True)]
  transfers between devices with their start and end apart: 3 -> 9, of which waited for: 3 -> 6; matrix products, arithmetic and copies ran while one was open for 1% -> 1% of each run, Pallas kernels for 0% -> 0%
where the time goes in v1:
time: 255 us
  waiting for transfers between devices  113 us (44%)
  matrix products  62.6 us (25%)
  other arithmetic  35.7 us (14%)
  starting transfers between devices  17.3 us (7%)
  between operations  13.7 us (5%)
  local copies, waits for them, and re-layouts  12.2 us (5%)
    reduce_scatter x1, waiting for transfers between devices, body(): lax.psum_scatter(project().astype(jnp.bfloat16), 'head', scatter_dimensio...  77.5 us
    ppermute x7, waiting for transfers between devices, body(): part = lax.ppermute(part, 'ctx', [(d, d ^ mask) for d in range(ways)])  31.3 us
    dot_general x2, matrix products, attend_block(): jnp.einsum('gqsk,skd->qgd', weights.astype(jnp.bfloat16), value_block, pr...  27.1 us
    dot_general x2, matrix products, attend_block(): jnp.einsum('qgd,skd->gqsk', query_block, key_block, preferred_element_typ...  26.6 us
    reduce_sum x2, other arithmetic, attend_block(): totals = jnp.sum(weights, axis=(2, 3))  25.8 us
    ppermute x7, starting transfers between devices, body(): part = lax.ppermute(part, 'ctx', [(d, d ^ mask) for d in range(ways)])  9.95 us
    dot_general x1, matrix products, project(): return jnp.dot(part_rows, final_mapping, preferred_element_type=jnp.float32)  8.93 us
    all_to_all x1, starting transfers between devices, body(): lax.all_to_all(coded.reshape(ctx_count, 1), 'ctx', split_axis=0, concat_a...  7.31 us
  transfers between devices with their start and end apart: 9, of which 6 were waited for; matrix products, arithmetic and copies ran while one was open for 1% of the time, Pallas kernels for 0%

profile of v1, /device:TPU:0, one launch (start us, length us, event | category | flops | bytes accessed | tf_op | source)
XLA Modules:
  0.0 254.9 jit_solution(13272840623716062041)
XLA Ops:
  6.5 0.8 copy.35
  7.3 0.8 broadcast_compare_fusion.1
  8.1 0.1 copy.34
  8.1 0.1 copy.33
  8.3 0.1 fusion.26
  8.4 0.7 copy.36
  9.0 7.3 %all-to-all-start = ((s32[8,1,1]{2,1,0:T(1,128)}), s32[8,1,1]{2,1,0:T(1,128)S(1)}, u32[]{:S(2)}, u32[]{:S(2)}) async-start(s32[8,1,1]{2,1,0:T(1,128)} %copy.36), calls=%async_computation | async-start | bytes 8192 | tf_op jit(solution)/shard_map/all_to_all | solution.py:55
  16.4 0.8 compare_select_fusion
  17.3 1.1 pad_maximum_fusion.1
  18.4 4.4 %all-to-all-done = s32[8,1,1]{2,1,0:T(1,128)S(1)} async-done(((s32[8,1,1]{2,1,0:T(1,128)}), s32[8,1,1]{2,1,0:T(1,128)S(1)}, u32[]{:S(2)}, u32[]{:S(2)}) %all-to-all-start) | async-done | bytes 64 | tf_op jit(solution)/shard_map/all_to_all | solution.py:55
  22.8 0.2 clamp_reduce_fusion
  23.0 2.1 gather_fusion
  25.2 1.9 broadcast_select_fusion
  27.1 1.0 dynamic-slice_bitcast_fusion.1
  28.1 0.6 collective-permute-start
  28.6 0.6 collective-permute-start.1
  29.2 0.1 compare_and_fusion.1
  29.3 2.4 collective-permute-start.2
  31.8 0.6 collective-permute-start.3
  32.3 2.4 collective-permute-start.4
  34.7 0.4 broadcast_in_dim.73
  35.2 0.7 collective-permute-start.5
  35.9 10.0 %collective-permute-done.1 = bf16[2,1,512,128]{3,2,1,0:T(8,128)(2,1)S(1)} collective-permute-done((bf16[2,1,512,128]{3,2,1,0:T(8,128)(2,1)}, bf16[2,1,512,128]{3,2,1,0:T(8,128)(2,1)S(1)}, u32[]{:S(2)}, u32[]{:S(2)}) %collective-permute-start.1) | collective-permute-done | bytes 262176 | tf_op jit(solution)/shard_map/ppermute | solution.py:71
  45.8 2.8 %collective-permute-start.6 = (bf16[2,1,512,128]{3,2,1,0:T(8,128)(2,1)S(1)}, bf16[2,1,512,128]{3,2,1,0:T(8,128)(2,1)S(1)}, u32[]{:S(2)}, u32[]{:S(2)}) collective-permute-start(bf16[2,1,512,128]{3,2,1,0:T(8,128)(2,1)S(1)} %get-tuple-element.80), channel_id=1, source_target_pairs={{0,28},{4,24},{8,20},{12,16},{16,12},{20,8},{24,4},{28,0},{1,29},{... | collective-permute-start | bytes 786440 | tf_op jit(solution)/shard_map/ppermute | solution.py:71
  48.7 1.3 collective-permute-done.2
  50.1 14.4 %collective-permute-done.3 = bf16[2,1,512,128]{3,2,1,0:T(8,128)(2,1)S(1)} collective-permute-done((bf16[2,1,512,128]{3,2,1,0:T(8,128)(2,1)}, bf16[2,1,512,128]{3,2,1,0:T(8,128)(2,1)S(1)}, u32[]{:S(2)}, u32[]{:S(2)}) %collective-permute-start.3) | collective-permute-done | bytes 262176 | tf_op jit(solution)/shard_map/ppermute | solution.py:71
  64.6 5.6 %collective-permute-done.4 = bf16[2,1,512,128]{3,2,1,0:T(8,128)(2,1)S(1)} collective-permute-done((bf16[2,1,512,128]{3,2,1,0:T(8,128)(2,1)S(1)}, bf16[2,1,512,128]{3,2,1,0:T(8,128)(2,1)S(1)}, u32[]{:S(2)}, u32[]{:S(2)}) %collective-permute-start.4) | collective-permute-done | bytes 262176 | tf_op jit(solution)/shard_map/ppermute | solution.py:71
  70.3 0.2 pad_maximum_fusion
  70.5 2.9 %gather_fusion.1 = bf16[14,2,512,128]{3,2,1,0:T(8,128)(2,1)} fusion(bf16[2,10,512,128]{3,2,1,0:T(8,128)(2,1)S(1)} %pad_maximum_fusion, s32[1024]{0:T(1024)S(1)} %pad_clamp_fusion), kind=kCustom, calls=%fused_computation.1 | custom fusion | bytes 7340088 | tf_op jit(solution)/shard_map/jit(_take)/gather | solution.py:84
  73.4 2.4 fusion.23
  75.8 2.3 slice_bitcast_fusion
  78.1 83.5 %while.10 = (s32[]{:T(128)}, bf16[2,512,4,128]{3,2,1,0:T(4,128)(2,1)S(1)}, bf16[2,7,512,128]{3,2,1,0:T(8,128)(2,1)}, pred[2,7]{1,0:T(4,128)(4,1)S(1)}, bf16[2,7,...) while((s32[]{:T(128)}, bf16[2,512,4,128]{3,2,1,0:T(4,128)(2,1)S(1)}, ...), condition=%wide.region_4.5_spmd, body=%wide.region_1.4_spmd.sunk | while | flops 3843289088 | bytes 109355664 | solution.py:86
  78.2 1.1 or_and_fusion.2
  79.3 0.2 constant_dynamic-slice_fusion.2
  79.5 13.3 %fusion.38 = (f32[4,512]{1,0:T(4,128)S(1)}, f32[7,512,512,4]{2,1,3,0:T(8,128)}) fusion(pred[512,7,512]{0,2,1:T(8,128)(4,1)S(1)} %or_and_fusion.2, bf16[1,512,4,128]{3,2,1,0:T(4,128)(2,1)S(1)} %constant_dynamic-slice_fusion.2, bf16[2,7,512,128]{3,2,1,0:T(8,128)(2,1)} %get-tuple-element.147, s32[]{:T(128)} %get-tuple-element.136), kind=kOutput, calls=%fused_computation.6.clone.1 | convolution fusion | flops 1901066240 | bytes 32645632 | tf_op jit(solution)/shard_map/while/body/eval_jaxpr/qgd,skd->gqsk/dot_general | solution.py:12
  92.8 12.9 %fusion.39 = f32[4,512]{1,0:T(4,128)S(1)} fusion(f32[7,512,512,4]{2,1,3,0:T(8,128)} %get-tuple-element.127, f32[4,512]{1,0:T(4,128)S(1)} %get-tuple-element.128, pred[512,7,512]{0,2,1:T(8,128)(4,1)S(1)} %or_and_fusion.2), kind=kLoop, calls=%fused_computation.4.clone.1 | loop fusion | flops 29358080 | bytes 31211520 | tf_op jit(solution)/shard_map/while/body/eval_jaxpr/reduce_sum | solution.py:23
  105.7 13.5 %fusion.40 = bf16[1,512,4,128]{1,3,2,0:T(8,128)(2,1)S(1)} fusion(f32[7,512,512,4]{2,1,3,0:T(8,128)} %get-tuple-element.127, f32[4,512]{1,0:T(4,128)S(1)} %get-tuple-element.128, pred[512,7,512]{0,2,1:T(8,128)(4,1)S(1)} %or_and_fusion.2, bf16[2,7,512,128]{3,2,1,0:T(8,128)(2,1)S(1)} %copy-done.1, s32[]{:T(128)} %get-tuple-element.136, ...), kind=kOutput, calls=%fused_computation.13.clone.1 | convolution fusion | flops 1908932608 | bytes 32653316 | tf_op jit(solution)/shard_map/while/body/eval_jaxpr/gqsk,skd->qgd/dot_general | solution.py:24
  119.3 0.3 copy.68
  119.6 0.2 constant_dynamic-update-slice_fusion.9
  120.0 1.1 or_and_fusion.2
  121.0 0.2 constant_dynamic-slice_fusion.2
  121.2 13.3 %fusion.38 = (f32[4,512]{1,0:T(4,128)S(1)}, f32[7,512,512,4]{2,1,3,0:T(8,128)}) fusion(pred[512,7,512]{0,2,1:T(8,128)(4,1)S(1)} %or_and_fusion.2, bf16[1,512,4,128]{3,2,1,0:T(4,128)(2,1)S(1)} %constant_dynamic-slice_fusion.2, bf16[2,7,512,128]{3,2,1,0:T(8,128)(2,1)} %get-tuple-element.147, s32[]{:T(128)} %get-tuple-element.136), kind=kOutput, calls=%fused_computation.6.clone.1 | convolution fusion | flops 1901066240 | bytes 32645632 | tf_op jit(solution)/shard_map/while/body/eval_jaxpr/qgd,skd->gqsk/dot_general | solution.py:12
  134.6 12.9 %fusion.39 = f32[4,512]{1,0:T(4,128)S(1)} fusion(f32[7,512,512,4]{2,1,3,0:T(8,128)} %get-tuple-element.127, f32[4,512]{1,0:T(4,128)S(1)} %get-tuple-element.128, pred[512,7,512]{0,2,1:T(8,128)(4,1)S(1)} %or_and_fusion.2), kind=kLoop, calls=%fused_computation.4.clone.1 | loop fusion | flops 29358080 | bytes 31211520 | tf_op jit(solution)/shard_map/while/body/eval_jaxpr/reduce_sum | solution.py:23
  147.5 13.5 %fusion.40 = bf16[1,512,4,128]{1,3,2,0:T(8,128)(2,1)S(1)} fusion(f32[7,512,512,4]{2,1,3,0:T(8,128)} %get-tuple-element.127, f32[4,512]{1,0:T(4,128)S(1)} %get-tuple-element.128, pred[512,7,512]{0,2,1:T(8,128)(4,1)S(1)} %or_and_fusion.2, bf16[2,7,512,128]{3,2,1,0:T(8,128)(2,1)S(1)} %copy-done.1, s32[]{:T(128)} %get-tuple-element.136, ...), kind=kOutput, calls=%fused_computation.13.clone.1 | convolution fusion | flops 1908932608 | bytes 32653316 | tf_op jit(solution)/shard_map/while/body/eval_jaxpr/gqsk,skd->qgd/dot_general | solution.py:24
  161.0 0.3 copy.68
  161.3 0.2 constant_dynamic-update-slice_fusion.9
  161.6 8.9 %convolution_convert_fusion = bf16[1024,4096]{1,0:T(8,128)(2,1)} fusion(bf16[512,4096]{1,0:T(8,128)(2,1)} %param.11, bf16[128,8,4,128]{3,2,1,0:T(4,128)(2,1)S(1)} %bitcast.127), kind=kOutput, calls=%fused_computation.28 | convolution fusion | flops 4299161600 | bytes 13631488 | tf_op jit(solution)/shard_map/dot_general | solution.py:93
  170.5 77.5 %reduce-scatter.2.cloned.1.call-done = bf16[256,4096]{1,0:T(8,128)(2,1)} async-done(((bf16[1024,4096]{1,0:T(8,128)(2,1)}), bf16[256,4096]{1,0:T(8,128)(2,1)}) %reduce-scatter.2.cloned.1.call-update) | async-done | bytes 2097168 | tf_op jit(solution)/shard_map/reduce_scatter | solution.py:95
  (44 shorter events, 0.7 us)
Async XLA Ops:
  9.0 13.7 %all-to-all-start = ((s32[8,1,1]{2,1,0:T(1,128)}), s32[8,1,1]{2,1,0:T(1,128)S(1)}, u32[]{:S(2)}, u32[]{:S(2)}) async-start(s32[8,1,1]{2,1,0:T(1,128)} %copy.36), calls=%async_computation | async-start | bytes 8192 | tf_op jit(solution)/shard_map/all_to_all | solution.py:55
  16.4 231.7 %reduce-scatter.2.cloned.1.call-start = ((), (), s32[]{:S(2)}) async-start(), calls=%async_computation.2 | async-start | bytes 10485760 | tf_op jit(solution)/shard_map/reduce_scatter | solution.py:95
  27.0 2.2 copy-start.4
  28.1 7.1 %collective-permute-start = (bf16[2,1,512,128]{3,2,1,0:T(8,128)(2,1)}, bf16[2,1,512,128]{3,2,1,0:T(8,128)(2,1)S(1)}, u32[]{:S(2)}, u32[]{:S(2)}) collective-permute-start(bf16[2,1,512,128]{3,2,1,0:T(8,128)(2,1)} %get-tuple-element.86), channel_id=1, source_target_pairs={{0,4},{4,0},{8,12},{12,8},{16,20},{20,16},{24,28},{28,24},{1,5},{5... | collective-permute-start | bytes 786440 | tf_op jit(solution)/shard_map/ppermute | solution.py:71
  28.6 17.2 %collective-permute-start.1 = (bf16[2,1,512,128]{3,2,1,0:T(8,128)(2,1)}, bf16[2,1,512,128]{3,2,1,0:T(8,128)(2,1)S(1)}, u32[]{:S(2)}, u32[]{:S(2)}) collective-permute-start(bf16[2,1,512,128]{3,2,1,0:T(8,128)(2,1)} %get-tuple-element.85), channel_id=1, source_target_pairs={{0,8},{4,12},{8,0},{12,4},{16,24},{20,28},{24,16},{28,20},{1,9},{5... | collective-permute-start | bytes 786440 | tf_op jit(solution)/shard_map/ppermute | solution.py:71
  29.3 20.7 %collective-permute-start.2 = (bf16[2,1,512,128]{3,2,1,0:T(8,128)(2,1)}, bf16[2,1,512,128]{3,2,1,0:T(8,128)(2,1)S(1)}, u32[]{:S(2)}, u32[]{:S(2)}) collective-permute-start(bf16[2,1,512,128]{3,2,1,0:T(8,128)(2,1)} %get-tuple-element.84), channel_id=1, source_target_pairs={{0,12},{4,8},{8,4},{12,0},{16,28},{20,24},{24,20},{28,16},{1,13},{... | collective-permute-start | bytes 786440 | tf_op jit(solution)/shard_map/ppermute | solution.py:71
  31.8 32.8 %collective-permute-start.3 = (bf16[2,1,512,128]{3,2,1,0:T(8,128)(2,1)}, bf16[2,1,512,128]{3,2,1,0:T(8,128)(2,1)S(1)}, u32[]{:S(2)}, u32[]{:S(2)}) collective-permute-start(bf16[2,1,512,128]{3,2,1,0:T(8,128)(2,1)} %get-tuple-element.83), channel_id=1, source_target_pairs={{0,16},{4,20},{8,24},{12,28},{16,0},{20,4},{24,8},{28,12},{1,17},{... | collective-permute-start | bytes 786440 | tf_op jit(solution)/shard_map/ppermute | solution.py:71
  32.3 37.8 %collective-permute-start.4 = (bf16[2,1,512,128]{3,2,1,0:T(8,128)(2,1)S(1)}, bf16[2,1,512,128]{3,2,1,0:T(8,128)(2,1)S(1)}, u32[]{:S(2)}, u32[]{:S(2)}) collective-permute-start(bf16[2,1,512,128]{3,2,1,0:T(8,128)(2,1)S(1)} %get-tuple-element.82), channel_id=1, source_target_pairs={{0,20},{4,16},{8,28},{12,24},{16,4},{20,0},{24,12},{28,8},{1,21},{... | collective-permute-start | bytes 786440 | tf_op jit(solution)/shard_map/ppermute | solution.py:71
  35.1 35.2 %copy-start.2 = (bf16[1024,1,128]{2,0,1:T(8,128)(2,1)S(1)}, bf16[1024,1,128]{2,0,1:T(8,128)(2,1)}, u32[]{:S(2)}) copy-start(bf16[1024,1,128]{2,0,1:T(8,128)(2,1)} %param.9) | copy-start | bytes 786436
  35.1 35.2 %copy-start.3 = (bf16[1024,1,128]{2,0,1:T(8,128)(2,1)S(1)}, bf16[1024,1,128]{2,0,1:T(8,128)(2,1)}, u32[]{:S(2)}) copy-start(bf16[1024,1,128]{2,0,1:T(8,128)(2,1)} %param.8) | copy-start | bytes 786436
  35.2 35.0 %collective-permute-start.5 = (bf16[2,1,512,128]{3,2,1,0:T(8,128)(2,1)S(1)}, bf16[2,1,512,128]{3,2,1,0:T(8,128)(2,1)S(1)}, u32[]{:S(2)}, u32[]{:S(2)}) collective-permute-start(bf16[2,1,512,128]{3,2,1,0:T(8,128)(2,1)S(1)} %get-tuple-element.81), channel_id=1, source_target_pairs={{0,24},{4,28},{8,16},{12,20},{16,8},{20,12},{24,0},{28,4},{1,25},{... | collective-permute-start | bytes 786440 | tf_op jit(solution)/shard_map/ppermute | solution.py:71
  45.8 24.4 %collective-permute-start.6 = (bf16[2,1,512,128]{3,2,1,0:T(8,128)(2,1)S(1)}, bf16[2,1,512,128]{3,2,1,0:T(8,128)(2,1)S(1)}, u32[]{:S(2)}, u32[]{:S(2)}) collective-permute-start(bf16[2,1,512,128]{3,2,1,0:T(8,128)(2,1)S(1)} %get-tuple-element.80), channel_id=1, source_target_pairs={{0,28},{4,24},{8,20},{12,16},{16,12},{20,8},{24,4},{28,0},{1,29},{... | collective-permute-start | bytes 786440 | tf_op jit(solution)/shard_map/ppermute | solution.py:71
  75.8 2.3 copy-start
  75.8 2.3 copy-start.5
  92.8 12.9 %copy-start.1 = (bf16[2,7,512,128]{3,2,1,0:T(8,128)(2,1)S(1)}, bf16[2,7,512,128]{3,2,1,0:T(8,128)(2,1)}, u32[]{:S(2)}) copy-start(bf16[2,7,512,128]{3,2,1,0:T(8,128)(2,1)} %get-tuple-element.145) | copy-start | bytes 5505028 | tf_op jit(solution)/shard_map/while
  134.6 12.9 %copy-start.1 = (bf16[2,7,512,128]{3,2,1,0:T(8,128)(2,1)S(1)}, bf16[2,7,512,128]{3,2,1,0:T(8,128)(2,1)}, u32[]{:S(2)}) copy-start(bf16[2,7,512,128]{3,2,1,0:T(8,128)(2,1)} %get-tuple-element.145) | copy-start | bytes 5505028 | tf_op jit(solution)/shard_map/while
Sparse Core Ops, SparseCore 0:
  170.6 77.3 reduce-scatter.1
